TPU v7x, 32 devices: a 4x4x1 block of a 4x4x8 slice. The times are simulated.
32 devices in a mesh: data: 1 (over z), time: 32 (over y, x, core).
Axes of the slice: x: 4, y: 4, z: 1, core: 2. Of those that a mesh axis runs over, the one named last changes fastest.
The devices are a block of a 4x4x8 slice.
Arguments:
- x_init: float32 [16, 256, 16], P('data')
- w_in: bfloat16 [16, 768], replicated
- w_out: bfloat16 [768, 16], replicated
- mod_scale: bfloat16 [64, 768], P('time')
- mod_shift: bfloat16 [64, 768], P('time')
- step_size: float32 [64], P('time')
- noise_inc: float32 [64, 16, 256, 16], P('time', 'data')
Outputs:
- output: float32 [64, 16, 256, 16], P('time', 'data')
All inputs are finite; a program needn't handle non-finite values.
Results may differ from a plain program's by a relative error of at most 0.001.
Values are sent between devices in bfloat16 or wider.
A program may use at most 768 MiB of HBM per device.

v0:
```python
import jax
import jax.numpy as jnp
from jax import lax
from jax.sharding import PartitionSpec as P

SWEEPS = 8


def local_drift(latents, w_in, w_out, scale_f, shift_f, step_size):
    pre_act = jnp.einsum("tbnc,cd->tbnd", latents.astype(jnp.bfloat16), w_in, preferred_element_type=jnp.float32)
    hidden = pre_act * scale_f[:, None, None, :] + shift_f[:, None, None, :]
    gelu_out = jax.nn.gelu(hidden, approximate=True).astype(jnp.bfloat16)
    proj_out = jnp.einsum("tbnd,dc->tbnc", gelu_out, w_out, preferred_element_type=jnp.float32)
    return proj_out * step_size[:, None, None, None]


def solution(mesh):
    n_time = mesh.shape["time"]
    shifts = [2 ** level for level in range(12) if 2 ** level < n_time]

    def body(x_init, w_in, w_out, mod_scale, mod_shift, step_size, noise_inc):
        scale_f = 1.0 + mod_scale.astype(jnp.float32)
        shift_f = mod_shift.astype(jnp.float32)
        latents = jnp.broadcast_to(x_init[None], noise_inc.shape)
        for sweep_num in range(SWEEPS):
            increments = local_drift(latents, w_in, w_out, scale_f, shift_f, step_size) + noise_inc
            running = jnp.cumsum(increments, axis=0)
            dev_total = running[-1]
            prefix = dev_total
            for distance in shifts:
                moved = lax.ppermute(prefix, "time", [(source, source + distance) for source in range(n_time - distance)])
                prefix = prefix + moved
            latents = x_init[None] + (prefix - dev_total)[None] + (running - increments)
        return latents

    return jax.shard_map(
        body,
        mesh=mesh,
        in_specs=(P("data"), P(), P(), P("time"), P("time"), P("time"), P("time", "data")),
        out_specs=P("time", "data"),
        check_vma=False,
    )
```

profile of v0, /device:TPU:112, one launch (start us, length us, event | category | flops | bytes accessed | tf_op | source)
XLA Modules:
  0.0 519.1 jit_solution(17399815264559519030)
XLA Ops:
  2.4 11.4 %fusion.99 = f32[2,16,256,16]{2,3,1,0:T(8,128)S(1)} fusion(f32[2,16,256,16]{2,3,1,0:T(8,128)} %param.13, f32[2,768]{1,0:T(2,128)S(1)} %convert_element_type.57, f32[2,768]{1,0:T(2,128)S(1)} %convert_add_fusion, f32[2]{0:T(128)} %param.12, bf16[16,256,16]{1,2,0:T(8,128)(2,1)S(1)} %convert_element_type.55, bf16[768,16]{0,1:T(8,128)(2,1)S(1)} %copy-done, ...), kind=kOutput, calls=%fused_computation.89 | convolution fusion | flops 472121344 | bytes 1241096 | tf_op jit(solution)/shard_map/tbnd,dc->tbnc/dot_general | solution.py:13
  27.2 8.4 %collective-permute-done.1 = f32[16,256,16]{1,2,0:T(8,128)S(1)} collective-permute-done((f32[16,256,16]{1,2,0:T(8,128)S(1)}, f32[16,256,16]{1,2,0:T(8,128)S(1)}, u32[]{:S(2)}, u32[]{:S(2)}) %collective-permute-start.1) | collective-permute-done | bytes 262176 | tf_op jit(solution)/shard_map/ppermute | solution.py:31
  37.7 8.7 %collective-permute-done.2 = f32[16,256,16]{1,2,0:T(8,128)S(1)} collective-permute-done((f32[16,256,16]{1,2,0:T(8,128)S(1)}, f32[16,256,16]{1,2,0:T(8,128)S(1)}, u32[]{:S(2)}, u32[]{:S(2)}) %collective-permute-start.2) | collective-permute-done | bytes 262176 | tf_op jit(solution)/shard_map/ppermute | solution.py:31
  67.8 10.6 %fusion.105 = f32[2,16,256,16]{2,3,1,0:T(8,128)S(1)} fusion(f32[2,16,256,16]{2,3,1,0:T(8,128)S(1)} %copy-done.2, f32[2,768]{1,0:T(2,128)S(1)} %convert_element_type.57, f32[2,768]{1,0:T(2,128)S(1)} %convert_add_fusion, f32[2,16,256,16]{2,3,1,0:T(8,128)S(1)} %fusion.224, f32[2,16,256,16]{2,3,1,0:T(8,128)S(1)} %fusion.99, ...), kind=kOutput, calls=%fused_computation.91 | convolution fusion | flops 472514560 | bytes 2420744 | tf_op jit(solution)/shard_map/tbnd,dc->tbnc/dot_general | solution.py:13
  91.8 8.4 %collective-permute-done.6 = f32[16,256,16]{1,2,0:T(8,128)S(1)} collective-permute-done((f32[16,256,16]{1,2,0:T(8,128)S(1)}, f32[16,256,16]{1,2,0:T(8,128)S(1)}, u32[]{:S(2)}, u32[]{:S(2)}) %collective-permute-start.6) | collective-permute-done | bytes 262176 | tf_op jit(solution)/shard_map/ppermute | solution.py:31
  102.3 8.7 %collective-permute-done.7 = f32[16,256,16]{1,2,0:T(8,128)S(1)} collective-permute-done((f32[16,256,16]{1,2,0:T(8,128)S(1)}, f32[16,256,16]{1,2,0:T(8,128)S(1)}, u32[]{:S(2)}, u32[]{:S(2)}) %collective-permute-start.7) | collective-permute-done | bytes 262176 | tf_op jit(solution)/shard_map/ppermute | solution.py:31
  113.0 9.1 %collective-permute-done.8 = f32[16,256,16]{1,2,0:T(8,128)S(1)} collective-permute-done((f32[16,256,16]{1,2,0:T(8,128)S(1)}, f32[16,256,16]{1,2,0:T(8,128)S(1)}, u32[]{:S(2)}, u32[]{:S(2)}) %collective-permute-start.8) | collective-permute-done | bytes 262176 | tf_op jit(solution)/shard_map/ppermute | solution.py:31
  132.1 10.6 %fusion.111 = f32[2,16,256,16]{2,3,1,0:T(8,128)S(1)} fusion(f32[2,16,256,16]{2,3,1,0:T(8,128)S(1)} %copy-done.2, f32[2,768]{1,0:T(2,128)S(1)} %convert_element_type.57, f32[2,768]{1,0:T(2,128)S(1)} %convert_add_fusion, f32[2,16,256,16]{2,3,1,0:T(8,128)S(1)} %fusion.225, f32[2,16,256,16]{2,3,1,0:T(8,128)S(1)} %fusion.105, ...), kind=kOutput, calls=%fused_computation.93 | convolution fusion | flops 472514560 | bytes 2420744 | tf_op jit(solution)/shard_map/tbnd,dc->tbnc/dot_general | solution.py:13
  156.1 8.4 %collective-permute-done.11 = f32[16,256,16]{1,2,0:T(8,128)S(1)} collective-permute-done((f32[16,256,16]{1,2,0:T(8,128)S(1)}, f32[16,256,16]{1,2,0:T(8,128)S(1)}, u32[]{:S(2)}, u32[]{:S(2)}) %collective-permute-start.11) | collective-permute-done | bytes 262176 | tf_op jit(solution)/shard_map/ppermute | solution.py:31
  166.5 8.7 %collective-permute-done.12 = f32[16,256,16]{1,2,0:T(8,128)S(1)} collective-permute-done((f32[16,256,16]{1,2,0:T(8,128)S(1)}, f32[16,256,16]{1,2,0:T(8,128)S(1)}, u32[]{:S(2)}, u32[]{:S(2)}) %collective-permute-start.12) | collective-permute-done | bytes 262176 | tf_op jit(solution)/shard_map/ppermute | solution.py:31
  177.3 9.1 %collective-permute-done.13 = f32[16,256,16]{1,2,0:T(8,128)S(1)} collective-permute-done((f32[16,256,16]{1,2,0:T(8,128)S(1)}, f32[16,256,16]{1,2,0:T(8,128)S(1)}, u32[]{:S(2)}, u32[]{:S(2)}) %collective-permute-start.13) | collective-permute-done | bytes 262176 | tf_op jit(solution)/shard_map/ppermute | solution.py:31
  196.3 10.6 %fusion.117 = f32[2,16,256,16]{2,3,1,0:T(8,128)S(1)} fusion(f32[2,16,256,16]{2,3,1,0:T(8,128)S(1)} %copy-done.2, f32[2,768]{1,0:T(2,128)S(1)} %convert_element_type.57, f32[2,768]{1,0:T(2,128)S(1)} %convert_add_fusion, f32[2,16,256,16]{2,3,1,0:T(8,128)S(1)} %fusion.226, f32[2,16,256,16]{2,3,1,0:T(8,128)S(1)} %fusion.111, ...), kind=kOutput, calls=%fused_computation.95 | convolution fusion | flops 472514560 | bytes 2420744 | tf_op jit(solution)/shard_map/tbnd,dc->tbnc/dot_general | solution.py:13
  220.3 8.4 %collective-permute-done.16 = f32[16,256,16]{1,2,0:T(8,128)S(1)} collective-permute-done((f32[16,256,16]{1,2,0:T(8,128)S(1)}, f32[16,256,16]{1,2,0:T(8,128)S(1)}, u32[]{:S(2)}, u32[]{:S(2)}) %collective-permute-start.16) | collective-permute-done | bytes 262176 | tf_op jit(solution)/shard_map/ppermute | solution.py:31
  230.8 8.7 %collective-permute-done.17 = f32[16,256,16]{1,2,0:T(8,128)S(1)} collective-permute-done((f32[16,256,16]{1,2,0:T(8,128)S(1)}, f32[16,256,16]{1,2,0:T(8,128)S(1)}, u32[]{:S(2)}, u32[]{:S(2)}) %collective-permute-start.17) | collective-permute-done | bytes 262176 | tf_op jit(solution)/shard_map/ppermute | solution.py:31
  241.5 9.1 %collective-permute-done.18 = f32[16,256,16]{1,2,0:T(8,128)S(1)} collective-permute-done((f32[16,256,16]{1,2,0:T(8,128)S(1)}, f32[16,256,16]{1,2,0:T(8,128)S(1)}, u32[]{:S(2)}, u32[]{:S(2)}) %collective-permute-start.18) | collective-permute-done | bytes 262176 | tf_op jit(solution)/shard_map/ppermute | solution.py:31
  260.6 10.6 %fusion.123 = f32[2,16,256,16]{2,3,1,0:T(8,128)S(1)} fusion(f32[2,16,256,16]{2,3,1,0:T(8,128)S(1)} %copy-done.2, f32[2,768]{1,0:T(2,128)S(1)} %convert_element_type.57, f32[2,768]{1,0:T(2,128)S(1)} %convert_add_fusion, f32[2,16,256,16]{2,3,1,0:T(8,128)S(1)} %fusion.227, f32[2,16,256,16]{2,3,1,0:T(8,128)S(1)} %fusion.117, ...), kind=kOutput, calls=%fused_computation.97 | convolution fusion | flops 472514560 | bytes 2420744 | tf_op jit(solution)/shard_map/tbnd,dc->tbnc/dot_general | solution.py:13
  284.6 8.4 %collective-permute-done.21 = f32[16,256,16]{1,2,0:T(8,128)S(1)} collective-permute-done((f32[16,256,16]{1,2,0:T(8,128)S(1)}, f32[16,256,16]{1,2,0:T(8,128)S(1)}, u32[]{:S(2)}, u32[]{:S(2)}) %collective-permute-start.21) | collective-permute-done | bytes 262176 | tf_op jit(solution)/shard_map/ppermute | solution.py:31
  295.1 8.7 %collective-permute-done.22 = f32[16,256,16]{1,2,0:T(8,128)S(1)} collective-permute-done((f32[16,256,16]{1,2,0:T(8,128)S(1)}, f32[16,256,16]{1,2,0:T(8,128)S(1)}, u32[]{:S(2)}, u32[]{:S(2)}) %collective-permute-start.22) | collective-permute-done | bytes 262176 | tf_op jit(solution)/shard_map/ppermute | solution.py:31
  305.8 9.1 %collective-permute-done.23 = f32[16,256,16]{1,2,0:T(8,128)S(1)} collective-permute-done((f32[16,256,16]{1,2,0:T(8,128)S(1)}, f32[16,256,16]{1,2,0:T(8,128)S(1)}, u32[]{:S(2)}, u32[]{:S(2)}) %collective-permute-start.23) | collective-permute-done | bytes 262176 | tf_op jit(solution)/shard_map/ppermute | solution.py:31
  324.9 10.6 %fusion.129 = f32[2,16,256,16]{2,3,1,0:T(8,128)S(1)} fusion(f32[2,16,256,16]{2,3,1,0:T(8,128)S(1)} %copy-done.2, f32[2,768]{1,0:T(2,128)S(1)} %convert_element_type.57, f32[2,768]{1,0:T(2,128)S(1)} %convert_add_fusion, f32[2,16,256,16]{2,3,1,0:T(8,128)S(1)} %fusion.228, f32[2,16,256,16]{2,3,1,0:T(8,128)S(1)} %fusion.123, ...), kind=kOutput, calls=%fused_computation.99 | convolution fusion | flops 472514560 | bytes 2420744 | tf_op jit(solution)/shard_map/tbnd,dc->tbnc/dot_general | solution.py:13
  348.9 8.4 %collective-permute-done.26 = f32[16,256,16]{1,2,0:T(8,128)S(1)} collective-permute-done((f32[16,256,16]{1,2,0:T(8,128)S(1)}, f32[16,256,16]{1,2,0:T(8,128)S(1)}, u32[]{:S(2)}, u32[]{:S(2)}) %collective-permute-start.26) | collective-permute-done | bytes 262176 | tf_op jit(solution)/shard_map/ppermute | solution.py:31
  359.3 8.7 %collective-permute-done.27 = f32[16,256,16]{1,2,0:T(8,128)S(1)} collective-permute-done((f32[16,256,16]{1,2,0:T(8,128)S(1)}, f32[16,256,16]{1,2,0:T(8,128)S(1)}, u32[]{:S(2)}, u32[]{:S(2)}) %collective-permute-start.27) | collective-permute-done | bytes 262176 | tf_op jit(solution)/shard_map/ppermute | solution.py:31
  370.1 9.1 %collective-permute-done.28 = f32[16,256,16]{1,2,0:T(8,128)S(1)} collective-permute-done((f32[16,256,16]{1,2,0:T(8,128)S(1)}, f32[16,256,16]{1,2,0:T(8,128)S(1)}, u32[]{:S(2)}, u32[]{:S(2)}) %collective-permute-start.28) | collective-permute-done | bytes 262176 | tf_op jit(solution)/shard_map/ppermute | solution.py:31
  389.1 10.6 %fusion.135 = f32[2,16,256,16]{2,3,1,0:T(8,128)S(1)} fusion(f32[2,16,256,16]{2,3,1,0:T(8,128)S(1)} %copy-done.2, f32[2,768]{1,0:T(2,128)S(1)} %convert_element_type.57, f32[2,768]{1,0:T(2,128)S(1)} %convert_add_fusion, f32[2,16,256,16]{2,3,1,0:T(8,128)S(1)} %fusion.229, f32[2,16,256,16]{2,3,1,0:T(8,128)S(1)} %fusion.129, ...), kind=kOutput, calls=%fused_computation.101 | convolution fusion | flops 472514560 | bytes 2420744 | tf_op jit(solution)/shard_map/tbnd,dc->tbnc/dot_general | solution.py:13
  413.1 8.4 %collective-permute-done.31 = f32[16,256,16]{1,2,0:T(8,128)S(1)} collective-permute-done((f32[16,256,16]{1,2,0:T(8,128)S(1)}, f32[16,256,16]{1,2,0:T(8,128)S(1)}, u32[]{:S(2)}, u32[]{:S(2)}) %collective-permute-start.31) | collective-permute-done | bytes 262176 | tf_op jit(solution)/shard_map/ppermute | solution.py:31
  423.6 8.7 %collective-permute-done.32 = f32[16,256,16]{1,2,0:T(8,128)S(1)} collective-permute-done((f32[16,256,16]{1,2,0:T(8,128)S(1)}, f32[16,256,16]{1,2,0:T(8,128)S(1)}, u32[]{:S(2)}, u32[]{:S(2)}) %collective-permute-start.32) | collective-permute-done | bytes 262176 | tf_op jit(solution)/shard_map/ppermute | solution.py:31
  434.3 9.1 %collective-permute-done.33 = f32[16,256,16]{1,2,0:T(8,128)S(1)} collective-permute-done((f32[16,256,16]{1,2,0:T(8,128)S(1)}, f32[16,256,16]{1,2,0:T(8,128)S(1)}, u32[]{:S(2)}, u32[]{:S(2)}) %collective-permute-start.33) | collective-permute-done | bytes 262176 | tf_op jit(solution)/shard_map/ppermute | solution.py:31
  453.4 10.6 %fusion.141 = f32[2,16,256,16]{2,3,1,0:T(8,128)S(1)} fusion(f32[2,16,256,16]{2,3,1,0:T(8,128)S(1)} %copy-done.2, f32[2,768]{1,0:T(2,128)S(1)} %convert_element_type.57, f32[2,768]{1,0:T(2,128)S(1)} %convert_add_fusion, f32[2,16,256,16]{2,3,1,0:T(8,128)S(1)} %fusion.230, f32[2,16,256,16]{2,3,1,0:T(8,128)S(1)} %fusion.135, ...), kind=kOutput, calls=%fused_computation.103 | convolution fusion | flops 472514560 | bytes 2420744 | tf_op jit(solution)/shard_map/tbnd,dc->tbnc/dot_general | solution.py:13
  477.4 8.4 %collective-permute-done.36 = f32[16,256,16]{1,2,0:T(8,128)S(1)} collective-permute-done((f32[16,256,16]{1,2,0:T(8,128)S(1)}, f32[16,256,16]{1,2,0:T(8,128)S(1)}, u32[]{:S(2)}, u32[]{:S(2)}) %collective-permute-start.36) | collective-permute-done | bytes 262176 | tf_op jit(solution)/shard_map/ppermute | solution.py:31
  487.9 8.7 %collective-permute-done.37 = f32[16,256,16]{1,2,0:T(8,128)S(1)} collective-permute-done((f32[16,256,16]{1,2,0:T(8,128)S(1)}, f32[16,256,16]{1,2,0:T(8,128)S(1)}, u32[]{:S(2)}, u32[]{:S(2)}) %collective-permute-start.37) | collective-permute-done | bytes 262176 | tf_op jit(solution)/shard_map/ppermute | solution.py:31
  498.6 9.1 %collective-permute-done.38 = f32[16,256,16]{1,2,0:T(8,128)S(1)} collective-permute-done((f32[16,256,16]{1,2,0:T(8,128)S(1)}, f32[16,256,16]{1,2,0:T(8,128)S(1)}, u32[]{:S(2)}, u32[]{:S(2)}) %collective-permute-start.38) | collective-permute-done | bytes 262176 | tf_op jit(solution)/shard_map/ppermute | solution.py:31
  509.1 8.5 %collective-permute-done.39 = f32[16,256,16]{1,2,0:T(8,128)S(1)} collective-permute-done((f32[16,256,16]{1,2,0:T(8,128)S(1)}, f32[16,256,16]{1,2,0:T(8,128)S(1)}, u32[]{:S(2)}, u32[]{:S(2)}) %collective-permute-start.39) | collective-permute-done | bytes 262176 | tf_op jit(solution)/shard_map/ppermute | solution.py:31
  (126 shorter events, 222.4 us)
Async XLA Ops:
  15.4 9.8 %collective-permute-start = (f32[16,256,16]{1,2,0:T(8,128)S(1)}, f32[16,256,16]{1,2,0:T(8,128)S(1)}, u32[]{:S(2)}, u32[]{:S(2)}) collective-permute-start(f32[16,256,16]{1,2,0:T(8,128)S(1)} %slice_bitcast_fusion.7), channel_id=1, source_target_pairs={{0,1},{1,2},{2,3},{3,4},{4,5},{5,6},{6,7},{7,8},{8,9},{9,10},{10,1... | collective-permute-start | bytes 786440 | tf_op jit(solution)/shard_map/ppermute | solution.py:31
  25.3 10.4 %collective-permute-start.1 = (f32[16,256,16]{1,2,0:T(8,128)S(1)}, f32[16,256,16]{1,2,0:T(8,128)S(1)}, u32[]{:S(2)}, u32[]{:S(2)}) collective-permute-start(f32[16,256,16]{1,2,0:T(8,128)S(1)} %fusion.216), channel_id=1, source_target_pairs={{0,2},{1,3},{2,4},{3,5},{4,6},{5,7},{6,8},{7,9},{8,10},{9,11},{10,... | collective-permute-start | bytes 786440 | tf_op jit(solution)/shard_map/ppermute | solution.py:31
  35.7 10.7 %collective-permute-start.2 = (f32[16,256,16]{1,2,0:T(8,128)S(1)}, f32[16,256,16]{1,2,0:T(8,128)S(1)}, u32[]{:S(2)}, u32[]{:S(2)}) collective-permute-start(f32[16,256,16]{1,2,0:T(8,128)S(1)} %add.352), channel_id=1, source_target_pairs={{0,4},{1,5},{2,6},{3,7},{4,8},{5,9},{6,10},{7,11},{8,12},{9,13},{1... | collective-permute-start | bytes 786440 | tf_op jit(solution)/shard_map/ppermute | solution.py:31
  46.5 11.2 %collective-permute-start.3 = (f32[16,256,16]{1,2,0:T(8,128)S(1)}, f32[16,256,16]{1,2,0:T(8,128)S(1)}, u32[]{:S(2)}, u32[]{:S(2)}) collective-permute-start(f32[16,256,16]{1,2,0:T(8,128)S(1)} %add.353), channel_id=1, source_target_pairs={{0,8},{1,9},{2,10},{3,11},{4,12},{5,13},{6,14},{7,15},{8,16},{9,17... | collective-permute-start | bytes 786440 | tf_op jit(solution)/shard_map/ppermute | solution.py:31
  57.8 9.9 %collective-permute-start.4 = (f32[16,256,16]{1,2,0:T(8,128)S(1)}, f32[16,256,16]{1,2,0:T(8,128)S(1)}, u32[]{:S(2)}, u32[]{:S(2)}) collective-permute-start(f32[16,256,16]{1,2,0:T(8,128)S(1)} %add.354), channel_id=1, source_target_pairs={{0,16},{1,17},{2,18},{3,19},{4,20},{5,21},{6,22},{7,23},{8,24},{9,... | collective-permute-start | bytes 786440 | tf_op jit(solution)/shard_map/ppermute | solution.py:31
  80.0 9.8 %collective-permute-start.5 = (f32[16,256,16]{1,2,0:T(8,128)S(1)}, f32[16,256,16]{1,2,0:T(8,128)S(1)}, u32[]{:S(2)}, u32[]{:S(2)}) collective-permute-start(f32[16,256,16]{1,2,0:T(8,128)S(1)} %slice_bitcast_fusion.6), channel_id=1, source_target_pairs={{0,1},{1,2},{2,3},{3,4},{4,5},{5,6},{6,7},{7,8},{8,9},{9,10},{10,1... | collective-permute-start | bytes 786440 | tf_op jit(solution)/shard_map/ppermute | solution.py:31
  89.9 10.4 %collective-permute-start.6 = (f32[16,256,16]{1,2,0:T(8,128)S(1)}, f32[16,256,16]{1,2,0:T(8,128)S(1)}, u32[]{:S(2)}, u32[]{:S(2)}) collective-permute-start(f32[16,256,16]{1,2,0:T(8,128)S(1)} %fusion.217), channel_id=1, source_target_pairs={{0,2},{1,3},{2,4},{3,5},{4,6},{5,7},{6,8},{7,9},{8,10},{9,11},{10,... | collective-permute-start | bytes 786440 | tf_op jit(solution)/shard_map/ppermute | solution.py:31
  100.3 10.7 %collective-permute-start.7 = (f32[16,256,16]{1,2,0:T(8,128)S(1)}, f32[16,256,16]{1,2,0:T(8,128)S(1)}, u32[]{:S(2)}, u32[]{:S(2)}) collective-permute-start(f32[16,256,16]{1,2,0:T(8,128)S(1)} %add.364), channel_id=1, source_target_pairs={{0,4},{1,5},{2,6},{3,7},{4,8},{5,9},{6,10},{7,11},{8,12},{9,13},{1... | collective-permute-start | bytes 786440 | tf_op jit(solution)/shard_map/ppermute | solution.py:31
  111.0 11.1 %collective-permute-start.8 = (f32[16,256,16]{1,2,0:T(8,128)S(1)}, f32[16,256,16]{1,2,0:T(8,128)S(1)}, u32[]{:S(2)}, u32[]{:S(2)}) collective-permute-start(f32[16,256,16]{1,2,0:T(8,128)S(1)} %add.365), channel_id=1, source_target_pairs={{0,8},{1,9},{2,10},{3,11},{4,12},{5,13},{6,14},{7,15},{8,16},{9,17... | collective-permute-start | bytes 786440 | tf_op jit(solution)/shard_map/ppermute | solution.py:31
  144.2 9.8 %collective-permute-start.10 = (f32[16,256,16]{1,2,0:T(8,128)S(1)}, f32[16,256,16]{1,2,0:T(8,128)S(1)}, u32[]{:S(2)}, u32[]{:S(2)}) collective-permute-start(f32[16,256,16]{1,2,0:T(8,128)S(1)} %slice_bitcast_fusion.5), channel_id=1, source_target_pairs={{0,1},{1,2},{2,3},{3,4},{4,5},{5,6},{6,7},{7,8},{8,9},{9,10},{10,1... | collective-permute-start | bytes 786440 | tf_op jit(solution)/shard_map/ppermute | solution.py:31
  154.1 10.4 %collective-permute-start.11 = (f32[16,256,16]{1,2,0:T(8,128)S(1)}, f32[16,256,16]{1,2,0:T(8,128)S(1)}, u32[]{:S(2)}, u32[]{:S(2)}) collective-permute-start(f32[16,256,16]{1,2,0:T(8,128)S(1)} %fusion.218), channel_id=1, source_target_pairs={{0,2},{1,3},{2,4},{3,5},{4,6},{5,7},{6,8},{7,9},{8,10},{9,11},{10,... | collective-permute-start | bytes 786440 | tf_op jit(solution)/shard_map/ppermute | solution.py:31
  164.6 10.7 %collective-permute-start.12 = (f32[16,256,16]{1,2,0:T(8,128)S(1)}, f32[16,256,16]{1,2,0:T(8,128)S(1)}, u32[]{:S(2)}, u32[]{:S(2)}) collective-permute-start(f32[16,256,16]{1,2,0:T(8,128)S(1)} %add.376), channel_id=1, source_target_pairs={{0,4},{1,5},{2,6},{3,7},{4,8},{5,9},{6,10},{7,11},{8,12},{9,13},{1... | collective-permute-start | bytes 786440 | tf_op jit(solution)/shard_map/ppermute | solution.py:31
  175.3 11.1 %collective-permute-start.13 = (f32[16,256,16]{1,2,0:T(8,128)S(1)}, f32[16,256,16]{1,2,0:T(8,128)S(1)}, u32[]{:S(2)}, u32[]{:S(2)}) collective-permute-start(f32[16,256,16]{1,2,0:T(8,128)S(1)} %add.377), channel_id=1, source_target_pairs={{0,8},{1,9},{2,10},{3,11},{4,12},{5,13},{6,14},{7,15},{8,16},{9,17... | collective-permute-start | bytes 786440 | tf_op jit(solution)/shard_map/ppermute | solution.py:31
  208.5 9.8 %collective-permute-start.15 = (f32[16,256,16]{1,2,0:T(8,128)S(1)}, f32[16,256,16]{1,2,0:T(8,128)S(1)}, u32[]{:S(2)}, u32[]{:S(2)}) collective-permute-start(f32[16,256,16]{1,2,0:T(8,128)S(1)} %slice_bitcast_fusion.4), channel_id=1, source_target_pairs={{0,1},{1,2},{2,3},{3,4},{4,5},{5,6},{6,7},{7,8},{8,9},{9,10},{10,1... | collective-permute-start | bytes 786440 | tf_op jit(solution)/shard_map/ppermute | solution.py:31
  218.4 10.4 %collective-permute-start.16 = (f32[16,256,16]{1,2,0:T(8,128)S(1)}, f32[16,256,16]{1,2,0:T(8,128)S(1)}, u32[]{:S(2)}, u32[]{:S(2)}) collective-permute-start(f32[16,256,16]{1,2,0:T(8,128)S(1)} %fusion.219), channel_id=1, source_target_pairs={{0,2},{1,3},{2,4},{3,5},{4,6},{5,7},{6,8},{7,9},{8,10},{9,11},{10,... | collective-permute-start | bytes 786440 | tf_op jit(solution)/shard_map/ppermute | solution.py:31
  228.8 10.7 %collective-permute-start.17 = (f32[16,256,16]{1,2,0:T(8,128)S(1)}, f32[16,256,16]{1,2,0:T(8,128)S(1)}, u32[]{:S(2)}, u32[]{:S(2)}) collective-permute-start(f32[16,256,16]{1,2,0:T(8,128)S(1)} %add.388), channel_id=1, source_target_pairs={{0,4},{1,5},{2,6},{3,7},{4,8},{5,9},{6,10},{7,11},{8,12},{9,13},{1... | collective-permute-start | bytes 786440 | tf_op jit(solution)/shard_map/ppermute | solution.py:31
  239.6 11.1 %collective-permute-start.18 = (f32[16,256,16]{1,2,0:T(8,128)S(1)}, f32[16,256,16]{1,2,0:T(8,128)S(1)}, u32[]{:S(2)}, u32[]{:S(2)}) collective-permute-start(f32[16,256,16]{1,2,0:T(8,128)S(1)} %add.389), channel_id=1, source_target_pairs={{0,8},{1,9},{2,10},{3,11},{4,12},{5,13},{6,14},{7,15},{8,16},{9,17... | collective-permute-start | bytes 786440 | tf_op jit(solution)/shard_map/ppermute | solution.py:31
  272.8 9.8 %collective-permute-start.20 = (f32[16,256,16]{1,2,0:T(8,128)S(1)}, f32[16,256,16]{1,2,0:T(8,128)S(1)}, u32[]{:S(2)}, u32[]{:S(2)}) collective-permute-start(f32[16,256,16]{1,2,0:T(8,128)S(1)} %slice_bitcast_fusion.3), channel_id=1, source_target_pairs={{0,1},{1,2},{2,3},{3,4},{4,5},{5,6},{6,7},{7,8},{8,9},{9,10},{10,1... | collective-permute-start | bytes 786440 | tf_op jit(solution)/shard_map/ppermute | solution.py:31
  282.6 10.4 %collective-permute-start.21 = (f32[16,256,16]{1,2,0:T(8,128)S(1)}, f32[16,256,16]{1,2,0:T(8,128)S(1)}, u32[]{:S(2)}, u32[]{:S(2)}) collective-permute-start(f32[16,256,16]{1,2,0:T(8,128)S(1)} %fusion.220), channel_id=1, source_target_pairs={{0,2},{1,3},{2,4},{3,5},{4,6},{5,7},{6,8},{7,9},{8,10},{9,11},{10,... | collective-permute-start | bytes 786440 | tf_op jit(solution)/shard_map/ppermute | solution.py:31
  293.1 10.7 %collective-permute-start.22 = (f32[16,256,16]{1,2,0:T(8,128)S(1)}, f32[16,256,16]{1,2,0:T(8,128)S(1)}, u32[]{:S(2)}, u32[]{:S(2)}) collective-permute-start(f32[16,256,16]{1,2,0:T(8,128)S(1)} %add.400), channel_id=1, source_target_pairs={{0,4},{1,5},{2,6},{3,7},{4,8},{5,9},{6,10},{7,11},{8,12},{9,13},{1... | collective-permute-start | bytes 786440 | tf_op jit(solution)/shard_map/ppermute | solution.py:31
  303.8 11.1 %collective-permute-start.23 = (f32[16,256,16]{1,2,0:T(8,128)S(1)}, f32[16,256,16]{1,2,0:T(8,128)S(1)}, u32[]{:S(2)}, u32[]{:S(2)}) collective-permute-start(f32[16,256,16]{1,2,0:T(8,128)S(1)} %add.401), channel_id=1, source_target_pairs={{0,8},{1,9},{2,10},{3,11},{4,12},{5,13},{6,14},{7,15},{8,16},{9,17... | collective-permute-start | bytes 786440 | tf_op jit(solution)/shard_map/ppermute | solution.py:31
  346.9 10.4 %collective-permute-start.26 = (f32[16,256,16]{1,2,0:T(8,128)S(1)}, f32[16,256,16]{1,2,0:T(8,128)S(1)}, u32[]{:S(2)}, u32[]{:S(2)}) collective-permute-start(f32[16,256,16]{1,2,0:T(8,128)S(1)} %fusion.221), channel_id=1, source_target_pairs={{0,2},{1,3},{2,4},{3,5},{4,6},{5,7},{6,8},{7,9},{8,10},{9,11},{10,... | collective-permute-start | bytes 786440 | tf_op jit(solution)/shard_map/ppermute | solution.py:31
  357.4 10.7 %collective-permute-start.27 = (f32[16,256,16]{1,2,0:T(8,128)S(1)}, f32[16,256,16]{1,2,0:T(8,128)S(1)}, u32[]{:S(2)}, u32[]{:S(2)}) collective-permute-start(f32[16,256,16]{1,2,0:T(8,128)S(1)} %add.412), channel_id=1, source_target_pairs={{0,4},{1,5},{2,6},{3,7},{4,8},{5,9},{6,10},{7,11},{8,12},{9,13},{1... | collective-permute-start | bytes 786440 | tf_op jit(solution)/shard_map/ppermute | solution.py:31
  368.1 11.1 %collective-permute-start.28 = (f32[16,256,16]{1,2,0:T(8,128)S(1)}, f32[16,256,16]{1,2,0:T(8,128)S(1)}, u32[]{:S(2)}, u32[]{:S(2)}) collective-permute-start(f32[16,256,16]{1,2,0:T(8,128)S(1)} %add.413), channel_id=1, source_target_pairs={{0,8},{1,9},{2,10},{3,11},{4,12},{5,13},{6,14},{7,15},{8,16},{9,17... | collective-permute-start | bytes 786440 | tf_op jit(solution)/shard_map/ppermute | solution.py:31
  401.3 9.8 %collective-permute-start.30 = (f32[16,256,16]{1,2,0:T(8,128)S(1)}, f32[16,256,16]{1,2,0:T(8,128)S(1)}, u32[]{:S(2)}, u32[]{:S(2)}) collective-permute-start(f32[16,256,16]{1,2,0:T(8,128)S(1)} %slice_bitcast_fusion.1), channel_id=1, source_target_pairs={{0,1},{1,2},{2,3},{3,4},{4,5},{5,6},{6,7},{7,8},{8,9},{9,10},{10,1... | collective-permute-start | bytes 786440 | tf_op jit(solution)/shard_map/ppermute | solution.py:31
  411.2 10.4 %collective-permute-start.31 = (f32[16,256,16]{1,2,0:T(8,128)S(1)}, f32[16,256,16]{1,2,0:T(8,128)S(1)}, u32[]{:S(2)}, u32[]{:S(2)}) collective-permute-start(f32[16,256,16]{1,2,0:T(8,128)S(1)} %fusion.222), channel_id=1, source_target_pairs={{0,2},{1,3},{2,4},{3,5},{4,6},{5,7},{6,8},{7,9},{8,10},{9,11},{10,... | collective-permute-start | bytes 786440 | tf_op jit(solution)/shard_map/ppermute | solution.py:31
  421.6 10.7 %collective-permute-start.32 = (f32[16,256,16]{1,2,0:T(8,128)S(1)}, f32[16,256,16]{1,2,0:T(8,128)S(1)}, u32[]{:S(2)}, u32[]{:S(2)}) collective-permute-start(f32[16,256,16]{1,2,0:T(8,128)S(1)} %add.424), channel_id=1, source_target_pairs={{0,4},{1,5},{2,6},{3,7},{4,8},{5,9},{6,10},{7,11},{8,12},{9,13},{1... | collective-permute-start | bytes 786440 | tf_op jit(solution)/shard_map/ppermute | solution.py:31
  432.4 11.1 %collective-permute-start.33 = (f32[16,256,16]{1,2,0:T(8,128)S(1)}, f32[16,256,16]{1,2,0:T(8,128)S(1)}, u32[]{:S(2)}, u32[]{:S(2)}) collective-permute-start(f32[16,256,16]{1,2,0:T(8,128)S(1)} %add.425), channel_id=1, source_target_pairs={{0,8},{1,9},{2,10},{3,11},{4,12},{5,13},{6,14},{7,15},{8,16},{9,17... | collective-permute-start | bytes 786440 | tf_op jit(solution)/shard_map/ppermute | solution.py:31
  465.6 9.8 %collective-permute-start.35 = (f32[16,256,16]{1,2,0:T(8,128)S(1)}, f32[16,256,16]{1,2,0:T(8,128)S(1)}, u32[]{:S(2)}, u32[]{:S(2)}) collective-permute-start(f32[16,256,16]{1,2,0:T(8,128)S(1)} %slice_bitcast_fusion), channel_id=1, source_target_pairs={{0,1},{1,2},{2,3},{3,4},{4,5},{5,6},{6,7},{7,8},{8,9},{9,10},{10,1... | collective-permute-start | bytes 786440 | tf_op jit(solution)/shard_map/ppermute | solution.py:31
  475.5 10.4 %collective-permute-start.36 = (f32[16,256,16]{1,2,0:T(8,128)S(1)}, f32[16,256,16]{1,2,0:T(8,128)S(1)}, u32[]{:S(2)}, u32[]{:S(2)}) collective-permute-start(f32[16,256,16]{1,2,0:T(8,128)S(1)} %fusion.223), channel_id=1, source_target_pairs={{0,2},{1,3},{2,4},{3,5},{4,6},{5,7},{6,8},{7,9},{8,10},{9,11},{10,... | collective-permute-start | bytes 786440 | tf_op jit(solution)/shard_map/ppermute | solution.py:31
  485.9 10.7 %collective-permute-start.37 = (f32[16,256,16]{1,2,0:T(8,128)S(1)}, f32[16,256,16]{1,2,0:T(8,128)S(1)}, u32[]{:S(2)}, u32[]{:S(2)}) collective-permute-start(f32[16,256,16]{1,2,0:T(8,128)S(1)} %add.436), channel_id=1, source_target_pairs={{0,4},{1,5},{2,6},{3,7},{4,8},{5,9},{6,10},{7,11},{8,12},{9,13},{1... | collective-permute-start | bytes 786440 | tf_op jit(solution)/shard_map/ppermute | solution.py:31
  496.6 11.1 %collective-permute-start.38 = (f32[16,256,16]{1,2,0:T(8,128)S(1)}, f32[16,256,16]{1,2,0:T(8,128)S(1)}, u32[]{:S(2)}, u32[]{:S(2)}) collective-permute-start(f32[16,256,16]{1,2,0:T(8,128)S(1)} %add.437), channel_id=1, source_target_pairs={{0,8},{1,9},{2,10},{3,11},{4,12},{5,13},{6,14},{7,15},{8,16},{9,17... | collective-permute-start | bytes 786440 | tf_op jit(solution)/shard_map/ppermute | solution.py:31
  (13 other events, 132.2 us)
where the time goes:
time: 528 us; the launch traced here: 519 us
  waiting for transfers between devices  338 us (64%)
  matrix products  85.5 us (16%)
  starting transfers between devices  76.9 us (15%)
  other arithmetic  17.6 us (3%)
    ppermute x40, waiting for transfers between devices, body(): lax.ppermute(prefix, 'time', [(source, source + distance) for source in r...  338 us
    dot_general x8, matrix products, local_drift(): jnp.einsum('tbnd,dc->tbnc', gelu_out, w_out, preferred_element_type=jnp.f...  85.5 us
    ppermute x40, starting transfers between devices, body(): lax.ppermute(prefix, 'time', [(source, source + distance) for source in r...  76.9 us
    another operation x8, other arithmetic, body(): running = jnp.cumsum(increments, axis=0)  12.4 us
  transfers between devices with their start and end apart: 40, of which 40 were waited for; matrix products, arithmetic and copies ran while one was open for 0% of the time, Pallas kernels for 0%

commit v1 on v0

v1 whole, which is shorter than its diff:
```python
import functools
import math

import jax
import jax.numpy as jnp
from jax import lax
from jax.experimental import pallas as pl
from jax.experimental.pallas import tpu as pltpu
from jax.sharding import PartitionSpec as P

SWEEPS = 8
UNROLL = 16
SLOTS = 4
LIN = 2.0 * math.sqrt(2.0 / math.pi)
CUB = 8.0 * 0.044715 * math.sqrt(2.0 / math.pi)
F32, BF16 = jnp.float32, jnp.bfloat16


def kernel(n, own, x0_hbm, w_in, w_out, scale, shift, step, noise_hbm, out_hbm, weights, rhs, gathered, turned, base_tab,
           scale_all, shift_all, step_all, noise_all, x_all, x0, run, staged, *rest):
    hid, act = rest[:SLOTS], rest[SLOTS:2 * SLOTS]
    send_mod, recv_mod, send_noise, recv_noise, send_out, recv_out, local_sem = rest[2 * SLOTS:]
    me = lax.axis_index("time")
    chan, hidden = w_in.shape
    tok = x0.shape[1]
    per_row = x0_hbm.shape[2] // tok

    def chunk(dev):
        return dev // per_row, pl.ds(pl.multiple_of((dev % per_row) * tok, tok), tok)

    my_row, my_cols = chunk(me)

    def peer(k):
        return lax.rem(me + k, n)

    barrier = pltpu.get_barrier_semaphore()

    @pl.loop(1, n)
    def _(k):
        pl.semaphore_signal(barrier, inc=1, device_id={"time": peer(k)}, device_id_type=pl.DeviceIdType.MESH)

    first = pltpu.make_async_copy(x0_hbm.at[my_row, :, my_cols], x0, local_sem.at[0])
    first.start()
    mine = pltpu.make_async_copy(noise_hbm.at[:, my_row, :, my_cols], noise_all.at[me], local_sem.at[1])
    mine.start()
    scale_all[me] = scale[...]
    shift_all[me] = shift[...]
    for s in range(own):
        step_all[me, s:s + 1, :] = jnp.full((1, tok), step[s], F32)
    gathered[...] = jnp.zeros_like(gathered)
    first.wait()
    mine.wait()
    pl.semaphore_wait(barrier, n - 1)

    def mod_copies(dst, src_dev, k):
        pairs = ((scale, scale_all), (shift, shift_all), (step_all.at[me], step_all))
        return [
            pltpu.make_async_remote_copy(src_ref=a, dst_ref=b.at[src_dev], send_sem=send_mod.at[i, k], recv_sem=recv_mod.at[i, src_dev],
                                         device_id={"time": dst}, device_id_type=pl.DeviceIdType.MESH)
            for i, (a, b) in enumerate(pairs)
        ]

    def noise_copy(dst, src_dev, k):
        row, cols = chunk(dst)
        return pltpu.make_async_remote_copy(src_ref=noise_hbm.at[:, row, :, cols], dst_ref=noise_all.at[src_dev], send_sem=send_noise.at[k],
                                            recv_sem=recv_noise.at[src_dev], device_id={"time": dst}, device_id_type=pl.DeviceIdType.MESH)

    def out_copy(dst, src_dev, k):
        row, cols = chunk(src_dev)
        return pltpu.make_async_remote_copy(src_ref=x_all.at[dst], dst_ref=out_hbm.at[:, row, :, cols], send_sem=send_out.at[k],
                                            recv_sem=recv_out.at[src_dev], device_id={"time": dst}, device_id_type=pl.DeviceIdType.MESH)

    @pl.loop(1, n)
    def _(k):
        for copy in mod_copies(peer(k), me, k):
            copy.start()

    @pl.loop(1, n)
    def _(k):
        noise_copy(peer(k), me, k).start()

    x_first = x0[...]
    xb = x_first.astype(BF16)
    block = jnp.concatenate([xb, xb, xb, jnp.ones_like(xb)], axis=0)
    nothing = jnp.zeros_like(block)
    both = jnp.concatenate([jnp.concatenate([block, nothing], axis=1), jnp.concatenate([nothing, block], axis=1)], axis=0)

    @pl.loop(0, n)
    def _(q):
        rhs[q] = both

    run[...] = x_first
    for u in range(UNROLL):
        for t in range(own):
            staged[u, t] = xb

    @pl.loop(1, n)
    def _(k):
        source = lax.rem(me - k + n, n)
        for copy in mod_copies(peer(k), source, k):
            copy.wait_recv()

    rows = 2 * own * n
    for p in range(n):
        gathered[2 * own * p:2 * own * p + own, :] = scale_all[p].astype(F32)
        gathered[2 * own * p + own:2 * own * (p + 1), :] = shift_all[p].astype(F32)
    gathered[rows:rows + chan, :] = w_in[...].astype(F32)
    gathered[rows + chan:rows + chan + 8, :] = jnp.ones((8, hidden), F32)
    turned[...] = jnp.transpose(gathered[...]).astype(BF16)

    width = 64
    depth = gathered.shape[0]
    k_id = lax.broadcasted_iota(jnp.int32, (depth, 2 * width), 0)
    lane = lax.broadcasted_iota(jnp.int32, (depth, 2 * width), 1)
    part = lane % width
    which = lane // width
    pick_w = (part < 3 * chan) & (k_id == rows + part % chan)
    lane_row = lax.broadcasted_iota(jnp.int32, (1, 2 * width), 1) % width
    base_tab[...] = 0.5 * jnp.dot(turned[...], jnp.where(pick_w, 1.0, 0.0).astype(BF16), preferred_element_type=F32) + jnp.where(
        lane_row == 3 * chan, 0.5, 0.0)
    low_mask = jnp.where((lane_row >= 2 * chan) & (lane_row < 3 * chan), 1.0, 0.0)
    target = jnp.where(part < chan, rows + chan, jnp.where(part < 3 * chan, which, jnp.where(part == 3 * chan, own + which, depth)))
    moving = jnp.where((part >= chan) & (part <= 3 * chan), 2 * own, 0)

    @pl.loop(0, n // 2)
    def _(q2):
        picks = [jnp.where(k_id == target + moving * (2 * q2 + j), 1.0, 0.0).astype(BF16) for j in range(2)]
        factor = jnp.dot(turned[...], jnp.concatenate(picks, axis=1), preferred_element_type=F32)
        for j in range(2):
            value = base_tab[...] * factor[:, 2 * width * j:2 * width * (j + 1)]
            high = value.astype(BF16).astype(F32)
            weights[2 * q2 + j] = (value - high * low_mask).astype(BF16)

    @pl.loop(1, n)
    def _(k):
        source = lax.rem(me - k + n, n)
        noise_copy(peer(k), source, k).wait_recv()

    def first_product(q, slot):
        hid[slot][...] = jnp.dot(weights[q], rhs[q], preferred_element_type=F32)

    def activate(slot):
        g = hid[slot][...]
        act[slot][...] = g * (1.0 + jnp.tanh(g * (LIN + CUB * (g * g))))

    def second_product(q, slot, u):
        drift = jnp.dot(w_out[...].astype(F32), act[slot][...], preferred_element_type=F32)
        x = jnp.where(q == 0, x0[...], run[...])
        for t in range(own):
            x_all[q, t] = x
            if u is not None:
                staged[u, t] = x.astype(BF16)
            x = x + (drift[:, tok * t:tok * (t + 1)] * step_all[q, t:t + 1, :] + noise_all[q, t])
        run[...] = x

    first_product(0, 0)
    first_product(1, 1)

    def trip(i, carry):
        base = i * UNROLL
        for u in range(UNROLL):
            q = lax.rem(base + 2 * n - 1 - UNROLL + u, n)
            for t in range(own):
                xb = staged[u, t]
                for j in range(3):
                    rhs[q, width * t + chan * j:width * t + chan * (j + 1), tok * t:tok * (t + 1)] = xb
        for u in range(UNROLL):
            second_product(lax.rem(base + n - 1 + u, n), (u - 1) % SLOTS, u)
            activate(u % SLOTS)
            first_product(lax.rem(base + u + 2, n), (u + 2) % SLOTS)
        return carry

    lax.fori_loop(0, SWEEPS * n // UNROLL, trip, 0)
    second_product(n - 1, (UNROLL - 1) % SLOTS, None)

    @pl.loop(1, n)
    def _(k):
        out_copy(peer(k), me, k).start()

    last = pltpu.make_async_copy(x_all.at[me], out_hbm.at[:, my_row, :, my_cols], local_sem.at[0])
    last.start()
    last.wait()

    @pl.loop(1, n)
    def _(k):
        source = lax.rem(me - k + n, n)
        out_copy(peer(k), source, k).wait_recv()

    @pl.loop(1, n)
    def _(k):
        for copy in mod_copies(peer(k), me, k):
            copy.wait_send()
        noise_copy(peer(k), me, k).wait_send()
        out_copy(peer(k), me, k).wait_send()


def solution(mesh):
    n = mesh.shape["time"]

    def body(x_init, w_in, w_out, mod_scale, mod_shift, step_size, noise_inc):
        own, batch, tokens, chan = noise_inc.shape
        hidden = w_in.shape[1]
        tok = batch * tokens // n
        vmem, hbm, smem = (pl.BlockSpec(memory_space=m) for m in (pltpu.VMEM, pl.ANY, pltpu.SMEM))
        out = pl.pallas_call(
            functools.partial(kernel, n, own),
            out_shape=jax.ShapeDtypeStruct((own, batch, chan, tokens), F32),
            in_specs=[hbm, vmem, vmem, vmem, vmem, smem, hbm],
            out_specs=hbm,
            scratch_shapes=[
                pltpu.VMEM((n, hidden, 128), BF16),
                pltpu.VMEM((n, 128, own * tok), BF16),
                pltpu.VMEM((256, hidden), F32),
                pltpu.VMEM((hidden, 256), BF16),
                pltpu.VMEM((hidden, 128), F32),
                pltpu.VMEM((n, own, hidden), BF16),
                pltpu.VMEM((n, own, hidden), BF16),
                pltpu.VMEM((n, own, tok), F32),
                pltpu.VMEM((n, own, chan, tok), F32),
                pltpu.VMEM((n, own, chan, tok), F32),
                pltpu.VMEM((chan, tok), F32),
                pltpu.VMEM((chan, tok), F32),
                pltpu.VMEM((UNROLL, own, chan, tok), BF16),
            ]
            + [pltpu.VMEM((hidden, own * tok), F32)] * SLOTS
            + [pltpu.VMEM((hidden, own * tok), F32)] * SLOTS
            + [
                pltpu.SemaphoreType.DMA((3, n)),
                pltpu.SemaphoreType.DMA((3, n)),
                pltpu.SemaphoreType.DMA((n,)),
                pltpu.SemaphoreType.DMA((n,)),
                pltpu.SemaphoreType.DMA((n,)),
                pltpu.SemaphoreType.DMA((n,)),
                pltpu.SemaphoreType.DMA((2,)),
            ],
            compiler_params=pltpu.CompilerParams(collective_id=0, has_side_effects=True, vmem_limit_bytes=56 * 1024 * 1024),
            name="picard",
        )(jnp.swapaxes(x_init, 1, 2), w_in, w_out.T, mod_scale, mod_shift, step_size, jnp.swapaxes(noise_inc, 2, 3))
        return jnp.swapaxes(out, 2, 3)

    return jax.shard_map(
        body,
        mesh=mesh,
        in_specs=(P("data"), P(), P(), P("time"), P("time"), P("time"), P("time", "data")),
        out_specs=P("time", "data"),
        check_vma=False,
    )
```

time: 528 us -> 94 us (0.18)
  the two profiles are of different devices: /device:TPU:112 before, /device:TPU:97 now
where the time goes in v1:
time: 94 us; the launch traced here: 93.8 us
  Pallas kernels  91.9 us (98%)
  local copies, waits for them, and re-layouts  1.87 us (2%)
    pallas_call x1, Pallas kernels, body(): pl.pallas_call(functools.partial(kernel, n, own), out_shape=jax.ShapeDtyp...  91.9 us

profile of v1, /device:TPU:97, one launch (start us, length us, event | category | flops | bytes accessed | tf_op | source)
XLA Modules:
  0.0 93.8 jit_solution(4571946081110668217)
XLA Ops:
  0.0 91.9 %picard.1 = f32[2,16,16,256]{3,2,1,0:T(8,128)} custom-call(f32[16,16,256]{2,1,0:T(8,128)} %bitcast.6, bf16[16,768]{1,0:T(8,128)(2,1)} %w_in.1, bf16[16,768]{1,0:T(8,128)(2,1)} %bitcast.7, bf16[2,768]{1,0:T(2,128)(2,1)} %scale.1, bf16[2,768]{1,0:T(2,128)(2,1)} %shift.1, f32[2]{0:T(128)} %step.1, f32[2,16,16,256]{3,2,1,0:T(8,128)} %bitcast.5), custom_call_target="tpu_custom_call" | custom-call | tf_op jit(solution)/shard_map/picard/pallas_call | solution.py:205
  91.9 1.9 %copy.9 = f32[2,16,256,16]{2,3,1,0:T(8,128)} copy(f32[2,16,256,16]{2,3,1,0:T(8,128)} %bitcast.4) | data formatting | bytes 1048576

commit v2 on v0

v2 whole, which is shorter than its diff:
```python
import functools
import math

import jax
import jax.numpy as jnp
from jax import lax
from jax.experimental import pallas as pl
from jax.experimental.pallas import tpu as pltpu
from jax.sharding import PartitionSpec as P

SWEEPS = 8
UNROLL = 16
SLOTS = 2
LIN = 2.0 * math.sqrt(2.0 / math.pi)
CUB = 8.0 * 0.044715 * math.sqrt(2.0 / math.pi)
F32, BF16 = jnp.float32, jnp.bfloat16


def kernel(n, own, x0_hbm, w_in, w_out, scale, shift, step, noise_hbm, out_hbm, weights, rhs, scale_all, shift_all, step_all, noise_all,
           drift_mine, x_all, x0, run, staged, *rest):
    hid, act = rest[:SLOTS], rest[SLOTS:2 * SLOTS]
    (send_scale, recv_scale, send_shift, recv_shift, send_step, recv_step, send_noise, recv_noise, send_out, recv_out, local_sem) = rest[2 * SLOTS:]
    me = lax.axis_index("time")
    chan, hidden = w_in.shape
    tok = x0.shape[1]
    width = 64
    per_row = x0_hbm.shape[2] // tok

    def chunk(dev):
        return dev // per_row, pl.ds(pl.multiple_of((dev % per_row) * tok, tok), tok)

    my_row, my_cols = chunk(me)

    def peer(k):
        return lax.rem(me + k, n)

    def source(k):
        return lax.rem(me - k + n, n)

    def remote(src, dst, send_sem, recv_sem, dev):
        return pltpu.make_async_remote_copy(src_ref=src, dst_ref=dst, send_sem=send_sem, recv_sem=recv_sem, device_id={"time": dev},
                                            device_id_type=pl.DeviceIdType.MESH)

    def scale_copy(dst, src_dev, k):
        return remote(scale, scale_all.at[src_dev], send_scale.at[k], recv_scale.at[src_dev], dst)

    def shift_copy(dst, src_dev, k):
        return remote(shift, shift_all.at[src_dev], send_shift.at[k], recv_shift.at[src_dev], dst)

    def step_copy(dst, src_dev, k):
        return remote(step_all.at[me], step_all.at[src_dev], send_step.at[k], recv_step.at[src_dev], dst)

    def noise_copy(dst, src_dev, k):
        row, cols = chunk(dst)
        return remote(noise_hbm.at[:, row, :, cols], noise_all.at[src_dev], send_noise.at[k], recv_noise.at[src_dev], dst)

    def out_copy(dst, src_dev, k):
        row, cols = chunk(src_dev)
        return remote(x_all.at[dst], out_hbm.at[:, row, :, cols], send_out.at[k], recv_out.at[src_dev], dst)

    barrier = pltpu.get_barrier_semaphore()

    @pl.loop(1, n)
    def _(k):
        pl.semaphore_signal(barrier, inc=1, device_id={"time": peer(k)}, device_id_type=pl.DeviceIdType.MESH)

    local = [
        pltpu.make_async_copy(x0_hbm.at[my_row, :, my_cols], x0, local_sem.at[0]),
        pltpu.make_async_copy(noise_hbm.at[:, my_row, :, my_cols], noise_all.at[me], local_sem.at[1]),
    ]
    for copy in local:
        copy.start()
    scale_all[me] = scale[...]
    shift_all[me] = shift[...]
    for t in range(own):
        step_all[me, t:t + 1, :] = jnp.full((1, tok), step[t], F32)

    half = 0.5 * w_in[...].astype(F32)
    top = lax.broadcasted_iota(jnp.int32, (chan, hidden), 0) == 0

    def modulated(scales, shifts):
        scales, shifts = scales.astype(F32), shifts.astype(F32)
        parts = []
        for t in range(own):
            value = half * scales[t:t + 1, :]
            high = value.astype(BF16)
            low = (value - high.astype(F32)).astype(BF16)
            bias = jnp.where(top, 0.5 * shifts[t:t + 1, :], 0.0).astype(BF16)
            parts += [half.astype(BF16), high, low, bias]
        return jnp.transpose(jnp.concatenate(parts, axis=0))

    for copy in local:
        copy.wait()

    xb = x0[...].astype(BF16)
    block = jnp.concatenate([xb, xb, xb, jnp.ones_like(xb)], axis=0)
    nothing = jnp.zeros_like(block)
    both = jnp.concatenate([jnp.concatenate([block, nothing], axis=1), jnp.concatenate([nothing, block], axis=1)], axis=0)

    @pl.loop(0, n)
    def _(q):
        rhs[q] = both

    def put_latents(q, t, xb):
        for j in range(3):
            rhs[q, width * t + chan * j:width * t + chan * (j + 1), tok * t:tok * (t + 1)] = xb

    def first_product(w, q, slot):
        right = rhs[q]
        for part in range(2):
            rows = slice(part * hidden // 2, (part + 1) * hidden // 2)
            hid[slot][rows, :] = jnp.dot(weights[w, rows, :], right, preferred_element_type=F32)

    def activate(slot):
        g = hid[slot][...]
        act[slot][...] = g * (1.0 + jnp.tanh(g * (LIN + CUB * (g * g))))

    def second_product(slot):
        return jnp.dot(w_out[...].astype(F32), act[slot][...], preferred_element_type=F32)

    def sweep(into):
        def finish(q, slot):
            drift = second_product(slot)
            for t in range(own):
                into[q, t] = drift[:, tok * t:tok * (t + 1)] * step_all[q, t:t + 1, :]

        weights[0] = modulated(scale_all[0], shift_all[0])
        first_product(0, 0, 0)

        def trip(i, carry):
            base = i * UNROLL
            for u in range(UNROLL):
                nxt = lax.rem(base + u + 1, n)
                weights[nxt] = modulated(scale_all[nxt], shift_all[nxt])
                finish(lax.rem(base + n - 1 + u, n), (u - 1) % SLOTS)
                activate(u % SLOTS)
                first_product(nxt, nxt, (u + 1) % SLOTS)
            return carry

        lax.fori_loop(0, n // UNROLL, trip, 0)
        finish(n - 1, (UNROLL - 1) % SLOTS)

    pl.semaphore_wait(barrier, n - 1)

    @pl.loop(1, n)
    def _(k):
        scale_copy(peer(k), me, k).start()
        shift_copy(peer(k), me, k).start()
        step_copy(peer(k), me, k).start()

    @pl.loop(1, n)
    def _(k):
        noise_copy(peer(k), me, k).start()

    @pl.loop(1, n)
    def _(k):
        scale_copy(peer(k), source(k), k).wait_recv()
        shift_copy(peer(k), source(k), k).wait_recv()

    @pl.loop(1, n)
    def _(k):
        step_copy(peer(k), source(k), k).wait_recv()

    sweep(drift_mine)

    @pl.loop(1, n)
    def _(k):
        noise_copy(peer(k), source(k), k).wait_recv()

    x = x0[...]
    for q in range(n):
        for t in range(own):
            xb = x.astype(BF16)
            put_latents(q, t, xb)
            if q >= n - 1 - UNROLL and q < n - 1:
                staged[q - (n - 1 - UNROLL), t] = xb
            if q == n - 1 and t == 0:
                run[...] = x
            x = x + (drift_mine[q, t] + noise_all[q, t])

    def advance(q, slot, u):
        change = second_product(slot)
        x = jnp.where(q == 0, x0[...], run[...])
        for t in range(own):
            x_all[q, t] = x
            if u is not None:
                staged[u, t] = x.astype(BF16)
            x = x + (change[:, tok * t:tok * (t + 1)] * step_all[q, t:t + 1, :] + noise_all[q, t])
        run[...] = x

    first_product(0, 0, 0)

    def trip(i, carry):
        base = i * UNROLL
        for u in range(UNROLL):
            late = lax.rem(base + 2 * n - 1 - UNROLL + u, n)
            for t in range(own):
                put_latents(late, t, staged[u, t])
            advance(lax.rem(base + n - 1 + u, n), (u - 1) % SLOTS, u)
            activate(u % SLOTS)
            q = lax.rem(base + u + 1, n)
            first_product(q, q, (u + 1) % SLOTS)
        return carry

    trips = (SWEEPS - 1) * n // UNROLL
    early = n - UNROLL - 1
    lax.fori_loop(0, trips - 1, trip, 0)

    def deliver(first_dev, count):
        @pl.loop(0, count)
        def _(k):
            dst = first_dev + lax.rem(me + k, count)

            @pl.when(dst != me)
            def _():
                out_copy(dst, me, lax.rem(dst - me + n, n)).start()

    deliver(0, early)
    trip(trips - 1, 0)
    advance(n - 1, (UNROLL - 1) % SLOTS, None)
    deliver(early, n - early)

    last = pltpu.make_async_copy(x_all.at[me], out_hbm.at[:, my_row, :, my_cols], local_sem.at[0])
    last.start()
    last.wait()

    @pl.loop(1, n)
    def _(k):
        out_copy(peer(k), source(k), k).wait_recv()

    @pl.loop(1, n)
    def _(k):
        scale_copy(peer(k), me, k).wait_send()
        shift_copy(peer(k), me, k).wait_send()
        step_copy(peer(k), me, k).wait_send()
        noise_copy(peer(k), me, k).wait_send()
        out_copy(peer(k), me, k).wait_send()


def solution(mesh):
    n = mesh.shape["time"]

    def body(x_init, w_in, w_out, mod_scale, mod_shift, step_size, noise_inc):
        own, batch, tokens, chan = noise_inc.shape
        hidden = w_in.shape[1]
        tok = batch * tokens // n
        vmem, hbm, smem = (pl.BlockSpec(memory_space=m) for m in (pltpu.VMEM, pl.ANY, pltpu.SMEM))
        out = pl.pallas_call(
            functools.partial(kernel, n, own),
            out_shape=jax.ShapeDtypeStruct((own, batch, chan, tokens), F32),
            in_specs=[hbm, vmem, vmem, vmem, vmem, smem, hbm],
            out_specs=hbm,
            scratch_shapes=[
                pltpu.VMEM((n, hidden, 128), BF16),
                pltpu.VMEM((n, 128, own * tok), BF16),
                pltpu.VMEM((n, own, hidden), BF16),
                pltpu.VMEM((n, own, hidden), BF16),
                pltpu.VMEM((n, own, tok), F32),
            ]
            + [pltpu.VMEM((n, own, chan, tok), F32)] * 3
            + [
                pltpu.VMEM((chan, tok), F32),
                pltpu.VMEM((chan, tok), F32),
                pltpu.VMEM((UNROLL, own, chan, tok), BF16),
            ]
            + [pltpu.VMEM((hidden, own * tok), F32)] * (2 * SLOTS)
            + [pltpu.SemaphoreType.DMA((n,))] * 10
            + [pltpu.SemaphoreType.DMA((2,))],
            compiler_params=pltpu.CompilerParams(collective_id=0, has_side_effects=True, vmem_limit_bytes=40 * 1024 * 1024),
            name="picard",
        )(jnp.swapaxes(x_init, 1, 2), w_in, w_out.T, mod_scale, mod_shift, step_size, jnp.swapaxes(noise_inc, 2, 3))
        return jnp.swapaxes(out, 2, 3)

    return jax.shard_map(
        body,
        mesh=mesh,
        in_specs=(P("data"), P(), P(), P("time"), P("time"), P("time"), P("time", "data")),
        out_specs=P("time", "data"),
        check_vma=False,
    )
```

time: 528 us -> 88.8 us (0.17); the launches traced: 519 us -> 88.3 us
  waiting for transfers between devices: 338 us -> 0 us
  matrix products: 85.5 us -> 0 us
  Pallas kernels: 0 us -> 82.6 us
  starting transfers between devices: 76.9 us -> 0 us
  other arithmetic: 17.6 us -> 0 us
  local copies, waits for them, and re-layouts: 0.18 us -> 5.63 us
    ppermute x40 -> x0, waiting for transfers between devices: 338 us -> none  [body(): lax.ppermute(prefix, 'time', [(source, source + distance) for source in r...]
    dot_general x8 -> x0, matrix products: 85.5 us -> none  [local_drift(): jnp.einsum('tbnd,dc->tbnc', gelu_out, w_out, preferred_element_type=jnp.f...]
    pallas_call x0 -> x1, Pallas kernels: none -> 82.6 us  [body(): pl.pallas_call(functools.partial(kernel, n, own), out_shape=jax.ShapeDtyp...]
    ppermute x40 -> x0, starting transfers between devices: 76.9 us -> none  [body(): lax.ppermute(prefix, 'time', [(source, source + distance) for source in r...]
    another operation x8 -> x0, other arithmetic: 12.4 us -> none  [body(): running = jnp.cumsum(increments, axis=0)]
    unnamed x10 -> x15, local copies, waits for them, and re-layouts: 0.03 us -> 5.63 us
  transfers between devices with their start and end apart: 40 -> 0, of which waited for: 40 -> 0; matrix products, arithmetic and copies ran while one was open for 0% -> 0% of each run, Pallas kernels for 0% -> 0%
where the time goes in v2:
time: 88.8 us; the launch traced here: 88.3 us
  Pallas kernels  82.6 us (93%)
  local copies, waits for them, and re-layouts  5.63 us (6%)
    pallas_call x1, Pallas kernels, body(): pl.pallas_call(functools.partial(kernel, n, own), out_shape=jax.ShapeDtyp...  82.6 us
    unnamed x15, local copies, waits for them, and re-layouts  5.63 us

profile of v2, /device:TPU:112, one launch (start us, length us, event | category | flops | bytes accessed | tf_op | source)
XLA Modules:
  0.0 88.3 jit_solution(17963301100461223423)
XLA Ops:
  0.0 0.0 copy-start.4
  0.0 0.0 copy-start.6
  0.0 0.7 copy-done.4
  0.7 0.0 copy-done.6
  0.7 0.0 copy-start
  0.7 1.0 %copy-done = f32[2,16,256,16]{2,3,1,0:T(8,128)S(1)} copy-done((f32[2,16,256,16]{2,3,1,0:T(8,128)S(1)}, f32[2,16,256,16]{2,3,1,0:T(8,128)}, u32[]{:S(2)}) %copy-start) | copy-done | bytes 524312
  1.7 0.0 copy-start.1
  1.7 0.9 %copy-done.1 = f32[16,256,16]{1,2,0:T(8,128)S(1)} copy-done((f32[16,256,16]{1,2,0:T(8,128)S(1)}, f32[16,256,16]{1,2,0:T(8,128)}, u32[]{:S(2)}) %copy-start.1) | copy-done | bytes 262168
  2.7 0.0 copy-start.2
  2.7 0.7 copy-done.2
  3.4 0.0 copy-start.3
  3.4 0.7 copy-done.3
  4.2 0.0 copy-start.5
  4.2 0.7 copy-done.5
  4.8 82.6 %picard.1 = f32[2,16,16,256]{3,2,1,0:T(8,128)S(1)} custom-call(f32[16,16,256]{2,1,0:T(8,128)S(1)} %bitcast.6, bf16[16,768]{1,0:T(8,128)(2,1)S(1)} %copy-done.2, bf16[16,768]{1,0:T(8,128)(2,1)S(1)} %bitcast.7, bf16[2,768]{1,0:T(2,128)(2,1)S(1)} %copy-done.4, bf16[2,768]{1,0:T(2,128)(2,1)S(1)} %copy-done.5, f32[2]{0:T(128)S(1)} %copy-done.6, ...), custom_call_target="tpu_custom_call" | custom-call | tf_op jit(solution)/shard_map/picard/pallas_call | solution.py:248
  87.5 0.8 copy.9
Async XLA Ops:
  0.0 0.7 copy-start.4
  0.0 0.7 copy-start.6
  0.7 1.0 %copy-start = (f32[2,16,256,16]{2,3,1,0:T(8,128)S(1)}, f32[2,16,256,16]{2,3,1,0:T(8,128)}, u32[]{:S(2)}) copy-start(f32[2,16,256,16]{2,3,1,0:T(8,128)} %param.13) | copy-start | bytes 1572868
  1.7 0.9 %copy-start.1 = (f32[16,256,16]{1,2,0:T(8,128)S(1)}, f32[16,256,16]{1,2,0:T(8,128)}, u32[]{:S(2)}) copy-start(f32[16,256,16]{1,2,0:T(8,128)} %param.7) | copy-start | bytes 786436
  2.7 0.7 copy-start.2
  3.4 0.7 copy-start.3
  4.2 0.7 copy-start.5
